TPU v7x, 16 devices: a 4x2x1 block of a 4x4x8 slice. The times are simulated.
16 devices in a mesh: dp: 2 (over y, z), tp: 8 (over x, core).
Axes of the slice: x: 4, y: 2, z: 1, core: 2. Of those that a mesh axis runs over, the one named last changes fastest.
The devices are a block of a 4x4x8 slice.
Arguments:
- x: bfloat16 [4096, 5120], P('dp'), parts along dimension 0
- w_gate: bfloat16 [5120, 32768], P(None, 'tp')
- w_up: bfloat16 [5120, 32768], P(None, 'tp')
- w_down: bfloat16 [32768, 5120], P('tp')
Outputs:
- output: bfloat16 [4096, 5120], P('dp'), parts along dimension 0
There are 2 independent parts. A program takes and returns all parts, laid end to end along the dimension named above; an argument that names none is the same for every part.
All inputs are finite; a program needn't handle non-finite values.
Results may differ from a plain program's by a relative error of at most 0.016.
Values are sent between devices in bfloat16 or wider.
A program may use at most 768 MiB of HBM per device.

v0:
```python
import jax
import jax.numpy as jnp
from jax import lax
from jax.sharding import PartitionSpec as P


def solution(mesh):
    def step(x, w_gate, w_up, w_down):
        gate = jnp.dot(x, w_gate, preferred_element_type=jnp.float32)
        up = jnp.dot(x, w_up, preferred_element_type=jnp.float32)
        hidden = (jax.nn.silu(gate) * up).astype(jnp.bfloat16)
        term = jnp.dot(hidden, w_down, preferred_element_type=jnp.float32).astype(jnp.bfloat16)
        return lax.psum(term, "tp")

    return jax.shard_map(
        step,
        mesh=mesh,
        in_specs=(P("dp", None), P(None, "tp"), P(None, "tp"), P("tp", None)),
        out_specs=P("dp", None),
        check_vma=False,
    )
```

profile of v0, /device:TPU:113, one launch (start us, length us, event | category | flops | bytes accessed | tf_op | source)
XLA Modules:
  0.0 545.5 jit_solution(16785793149739972035)
XLA Ops:
  6.5 0.0 all-reduce.2.cloned.1.call-start
  6.6 96.8 %fusion = f32[2048,4096]{1,0:T(8,128)} fusion(bf16[2048,5120]{1,0:T(8,128)(2,1)} %param.4, bf16[5120,4096]{1,0:T(8,128)(2,1)} %param.5), kind=kOutput, calls=%fused_computation.2 | convolution fusion | flops 85899345920 | bytes 96468992 | tf_op jit(solution)/shard_map/dot_general | solution.py:9
  103.3 105.4 %multiply_convert_fusion = bf16[2048,4096]{1,0:T(8,128)(2,1)} fusion(f32[2048,4096]{1,0:T(8,128)} %fusion, bf16[2048,5120]{1,0:T(8,128)(2,1)} %param.4, bf16[5120,4096]{1,0:T(8,128)(2,1)} %param.6), kind=kOutput, calls=%fused_computation | convolution fusion | flops 85949677568 | bytes 113246208 | tf_op jit(solution)/shard_map/dot_general | solution.py:10
  208.7 95.9 %convolution_convert_fusion = bf16[2048,5120]{1,0:T(8,128)(2,1)} fusion(bf16[2048,4096]{1,0:T(8,128)(2,1)} %multiply_convert_fusion, bf16[4096,5120]{1,0:T(8,128)(2,1)} %param.7), kind=kOutput, calls=%fused_computation.1 | convolution fusion | flops 85909831680 | bytes 79691776 | tf_op jit(solution)/shard_map/dot_general | solution.py:12
  304.6 0.1 all-reduce.2.cloned.1.call-update
  304.6 216.7 %all-reduce.2.cloned.1.call-done = bf16[2048,5120]{1,0:T(8,128)(2,1)} async-done(((bf16[2048,5120]{1,0:T(8,128)(2,1)}), bf16[2048,5120]{1,0:T(8,128)(2,1)}) %all-reduce.2.cloned.1.call-update) | async-done | bytes 20971536 | tf_op jit(solution)/shard_map/psum | solution.py:13
  521.4 17.3 %copy.6 = bf16[2048,5120]{1,0:T(8,128)(2,1)} copy(bf16[2048,5120]{1,0:T(8,128)(2,1)} %all-reduce.2.cloned.1.call-done) | data formatting | bytes 41943040
Async XLA Ops:
  6.5 514.8 %all-reduce.2.cloned.1.call-start = ((), (), s32[]{:S(2)}) async-start(), calls=%async_computation | async-start | bytes 41943040 | tf_op jit(solution)/shard_map/psum | solution.py:13
Sparse Core Ops, SparseCore 0:
  304.7 216.5 all-reduce.1
where the time goes:
time: 546 us
  matrix products  298 us (55%)
  waiting for transfers between devices  217 us (40%)
  local copies, waits for them, and re-layouts  17.3 us (3%)
  between operations  13.4 us (2%)
    psum x1, waiting for transfers between devices, step(): return lax.psum(term, 'tp')  217 us
    dot_general x1, matrix products, step(): up = jnp.dot(x, w_up, preferred_element_type=jnp.float32)  105 us
    dot_general x1, matrix products, step(): gate = jnp.dot(x, w_gate, preferred_element_type=jnp.float32)  96.8 us
    dot_general x1, matrix products, step(): jnp.dot(hidden, w_down, preferred_element_type=jnp.float32)  95.9 us
    unnamed x1, local copies, waits for them, and re-layouts  17.3 us
  transfers between devices with their start and end apart: 1, of which 1 were waited for; matrix products, arithmetic and copies ran while one was open for 0% of the time, Pallas kernels for 0%

commit v1 on v0

v1 whole, which is shorter than its diff:
```python
import functools

import jax
import jax.numpy as jnp
from jax import lax
from jax.experimental import pallas as pl
from jax.experimental.pallas import tpu as pltpu
from jax.sharding import PartitionSpec as P

CHUNK = 512
TILE = 512
MESH = pl.DeviceIdType.MESH
F32, BF16 = jnp.float32, jnp.bfloat16


def kernel(
    n, x_hbm, wg_hbm, wu_hbm, wd_hbm, y_hbm, far_hbm,
    x_buf, w_buf, hid, term, first, got, done,
    x_sem, w_sem, far_send, far_recv, hid_send, hid_recv,
    rs_send, rs_recv, ag_send, ag_recv, twin_send, local_sem, late_send, late_recv,
):
    ring = n // 2
    rows, depth = x_hbm.shape
    width = wg_hbm.shape[1]
    half = depth // 2
    chunks, ups, downs = rows // CHUNK, width // TILE, half // TILE
    steps = ups + downs
    piece, lanes = CHUNK // ring, TILE // 2

    me = lax.axis_index("tp")
    chip, core = me // 2, me % 2
    twin = me + 1 - 2 * core
    right, left = (me + 2) % n, (me + n - 2) % n
    towards = (right, left)

    barrier = pltpu.get_barrier_semaphore()
    for peer in (left, right, twin):
        pl.semaphore_signal(barrier, inc=1, device_id={"tp": peer}, device_id_type=MESH)
    pl.semaphore_wait(barrier, 3)

    def remote(src, dst, send, recv, peer):
        return pltpu.make_async_remote_copy(
            src_ref=src, dst_ref=dst, send_sem=send, recv_sem=recv,
            device_id={"tp": peer}, device_id_type=MESH,
        )

    def far_copy(u):
        cols = pl.multiple_of((1 - core) * half + u * TILE, TILE)
        return remote(
            wd_hbm.at[:, pl.ds(cols, TILE)], far_hbm.at[:, pl.ds(pl.multiple_of(u * TILE, TILE), TILE)],
            far_send.at[u], far_recv.at[u], twin,
        )

    def x_copy(k):
        at = pl.multiple_of(k * CHUNK, CHUNK)
        return pltpu.make_async_copy(x_hbm.at[pl.ds(at, CHUNK), :], x_buf, x_sem)

    def up_copies(i, slot):
        cols = pl.ds(pl.multiple_of(i * TILE, TILE), TILE)
        return (
            pltpu.make_async_copy(wg_hbm.at[:, cols], w_buf.at[slot, pl.ds(0, depth)], w_sem.at[slot, 0]),
            pltpu.make_async_copy(wu_hbm.at[:, cols], w_buf.at[slot, pl.ds(depth, depth)], w_sem.at[slot, 1]),
        )

    def down_copies(u, slot):
        cols = pl.ds(pl.multiple_of(core * half + u * TILE, TILE), TILE)
        far = pl.ds(pl.multiple_of(u * TILE, TILE), TILE)
        return (
            pltpu.make_async_copy(wd_hbm.at[:, cols], w_buf.at[slot, pl.ds(0, width)], w_sem.at[slot, 0]),
            pltpu.make_async_copy(far_hbm.at[:, far], w_buf.at[slot, pl.ds(width, width)], w_sem.at[slot, 1]),
        )

    def start(copies):
        for copy in copies:
            copy.start()

    def wait(copies):
        for copy in copies:
            copy.wait()

    def start_down(k, u, slot):
        @pl.when(k == 0)
        def _():
            far_copy(u).wait()

        start(down_copies(u, slot))

    def spot(k, u, d, owner):
        at = pl.multiple_of(k * CHUNK + owner * piece, piece)
        cols = pl.multiple_of(core * half + u * TILE + d * lanes, lanes)
        return y_hbm.at[pl.ds(at, piece), pl.ds(cols, lanes)]

    def owner_of(d, s):
        return (chip + ring - 1 - s) % ring if d == 0 else (chip + 1 + s) % ring

    def rs_copy(d, u, s):
        src = first.at[d, u] if s == 0 else got.at[d, u, s - 1]
        return remote(src, got.at[d, u, s], rs_send.at[d, u, s], rs_recv.at[d, u, s], towards[d])

    def ag_copy(k, d, u, s):
        owner = owner_of(d, ring - 1 + s)
        src = done.at[d, u] if s == 0 else spot(k, u, d, owner)
        return remote(src, spot(k, u, d, owner), ag_send.at[d, u, s], ag_recv.at[d, u, s], towards[d])

    def twin_copy(k, d, u, s):
        owner = owner_of(d, ring - 1 + s)
        src = done.at[d, u] if s == 0 else spot(k, u, d, owner)
        send = twin_send.at[d, u] if s == 0 else late_send
        return remote(src, spot(k, u, d, owner), send, late_recv, twin)

    def local_copy(k, d, u):
        return pltpu.make_async_copy(done.at[d, u], spot(k, u, d, chip), local_sem.at[d, u])

    def own_term(d, u, s):
        at = pl.multiple_of(owner_of(d, s) * piece, piece)
        return term[u, pl.ds(at, piece), pl.ds(d * lanes, lanes)]

    last = ring - 1

    def event(k, u, s):
        if s == 0:
            for d in range(2):
                first[d, u] = own_term(d, u, 0).astype(BF16)
            for d in range(2):
                rs_copy(d, u, 0).start()
        elif s < last:
            for d in range(2):
                rs_copy(d, u, s - 1).wait_recv()
                got[d, u, s - 1] = (got[d, u, s - 1].astype(F32) + own_term(d, u, s)).astype(BF16)
            for d in range(2):
                rs_copy(d, u, s).start()
        elif s == last:
            for d in range(2):
                rs_copy(d, u, s - 1).wait_recv()
                done[d, u] = (got[d, u, s - 1].astype(F32) + own_term(d, u, s)).astype(BF16)
                for r in range(last):
                    rs_copy(d, u, r).wait_send()
            for d in range(2):
                ag_copy(k, d, u, 0).start()
                twin_copy(k, d, u, 0).start()
                local_copy(k, d, u).start()
        else:
            for d in range(2):
                ag_copy(k, d, u, s - last - 1).wait_recv()
                if s < 2 * last:
                    ag_copy(k, d, u, s - last).start()
                twin_copy(k, d, u, s - last).start()
            if s == 2 * last:
                for d in range(2):
                    for r in range(last):
                        ag_copy(k, d, u, r).wait_send()
                    twin_copy(k, d, u, 0).wait_send()
                    local_copy(k, d, u).wait()

    def events(k, tau):
        for s in range(2 * last, -1, -1):
            u = tau - 2 * s

            @pl.when((u >= 0) & (u < downs))
            def _(u=u, s=s):
                event(k, u, s)

    start(up_copies(0, 0))
    x_copy(0).start()
    for u in range(downs):
        far_copy(u).start()

    def chunk_body(k, _):
        x_copy(k).wait()
        par = k % 2
        hid_here = hid.at[par]

        def hid_copy(i):
            own = pl.ds(pl.multiple_of(i * TILE, TILE), TILE)
            far = pl.ds(pl.multiple_of(width + i * TILE, TILE), TILE)
            return remote(hid.at[par, :, own], hid.at[par, :, far], hid_send.at[par], hid_recv.at[par], twin)

        def up_body(i, _):
            slot = (k * steps + i) % 2
            wait(up_copies(i, slot))

            @pl.when(i < ups - 1)
            def _():
                start(up_copies(i + 1, 1 - slot))

            @pl.when(i == ups - 1)
            def _():
                start_down(k, 0, 1 - slot)

            gate = jnp.dot(x_buf[...], w_buf[slot, pl.ds(0, depth)], preferred_element_type=F32)
            up = jnp.dot(x_buf[...], w_buf[slot, pl.ds(depth, depth)], preferred_element_type=F32)
            hid[par, :, pl.ds(pl.multiple_of(i * TILE, TILE), TILE)] = (jax.nn.silu(gate) * up).astype(BF16)

            @pl.when(k > 0)
            def _():
                events(k - 1, i + downs)

            hid_copy(i).start()
            return _

        lax.fori_loop(0, ups, up_body, None)

        @pl.when(k < chunks - 1)
        def _():
            x_copy(k + 1).start()

        whole = remote(
            hid.at[par, :, pl.ds(0, width)], hid.at[par, :, pl.ds(width, width)],
            hid_send.at[par], hid_recv.at[par], twin,
        )
        whole.wait()

        def down_body(u, _):
            slot = (k * steps + ups + u) % 2
            wait(down_copies(u, slot))

            @pl.when(u < downs - 1)
            def _():
                start_down(k, u + 1, 1 - slot)

            @pl.when((u == downs - 1) & (k < chunks - 1))
            def _():
                start(up_copies(0, 1 - slot))

            term[u] = jnp.dot(hid_here[...], w_buf[slot, pl.ds(0, 2 * width)], preferred_element_type=F32)

            @pl.when(k > 0)
            def _():
                events(k - 1, u + steps)

            events(k, u)
            return _

        lax.fori_loop(0, downs, down_body, None)
        return _

    lax.fori_loop(0, chunks, chunk_body, None)

    def tail(tau, _):
        events(chunks - 1, tau)
        return _

    lax.fori_loop(downs, downs + 4 * last, tail, None)

    share = (rows // ring) * last
    pltpu.make_async_copy(
        y_hbm.at[pl.ds(0, share), pl.ds(0, half)], y_hbm.at[pl.ds(0, share), pl.ds(0, half)], late_send
    ).wait()
    pltpu.make_async_copy(y_hbm.at[:, pl.ds(0, half)], y_hbm.at[:, pl.ds(0, half)], late_recv).wait()


def solution(mesh):
    n = mesh.shape["tp"]
    ring = n // 2

    def step(x, w_gate, w_up, w_down):
        rows, depth = x.shape
        width = w_gate.shape[1]
        half = depth // 2
        downs = half // TILE
        piece, lanes = CHUNK // ring, TILE // 2
        dma = pltpu.SemaphoreType.DMA
        y, _ = pl.pallas_call(
            functools.partial(kernel, n),
            name="mlp",
            out_shape=(
                jax.ShapeDtypeStruct((rows, depth), BF16),
                jax.ShapeDtypeStruct((width, half), BF16),
            ),
            in_specs=[pl.BlockSpec(memory_space=pl.ANY)] * 4,
            out_specs=[pl.BlockSpec(memory_space=pl.ANY)] * 2,
            scratch_shapes=[
                pltpu.VMEM((CHUNK, depth), BF16),
                pltpu.VMEM((2, 2 * depth, TILE), BF16),
                pltpu.VMEM((2, CHUNK, 2 * width), BF16),
                pltpu.VMEM((downs, CHUNK, TILE), F32),
                pltpu.VMEM((2, downs, piece, lanes), BF16),
                pltpu.VMEM((2, downs, ring - 1, piece, lanes), BF16),
                pltpu.VMEM((2, downs, piece, lanes), BF16),
                dma,
                dma((2, 2)),
                dma((downs,)),
                dma((downs,)),
                dma((2,)),
                dma((2,)),
                dma((2, downs, ring - 1)),
                dma((2, downs, ring - 1)),
                dma((2, downs, ring - 1)),
                dma((2, downs, ring - 1)),
                dma((2, downs)),
                dma((2, downs)),
                dma,
                dma,
            ],
            compiler_params=pltpu.CompilerParams(
                collective_id=0, has_side_effects=True, vmem_limit_bytes=67_043_328
            ),
            cost_estimate=pl.CostEstimate(
                flops=6 * rows * depth * width,
                bytes_accessed=2 * (2 * rows * depth + 12 * depth * width),
                transcendentals=rows * width,
            ),
        )(x, w_gate, w_up, w_down)
        return y

    return jax.shard_map(
        step,
        mesh=mesh,
        in_specs=(P("dp", None), P(None, "tp"), P(None, "tp"), P("tp", None)),
        out_specs=P("dp", None),
        check_vma=False,
    )
```

time: 546 us -> 356 us (0.65)
  Pallas kernels: 0 us -> 339 us
  matrix products: 298 us -> 0 us
  waiting for transfers between devices: 217 us -> 0 us
  between operations: 13.4 us -> 0.01 us
    pallas_call x0 -> x1, Pallas kernels: none -> 339 us  [step(): pl.pallas_call(functools.partial(kernel, n), name='mlp', out_shape=(jax.S...]
    dot_general x3 -> x0, matrix products: 298 us -> none  [the longest x1 105 us: step(): up = jnp.dot(x, w_up, preferred_element_type=jnp.float32)]
    psum x1 -> x0, waiting for transfers between devices: 217 us -> none  [step(): return lax.psum(term, 'tp')]
  transfers between devices with their start and end apart: 1 -> 0, of which waited for: 1 -> 0; matrix products, arithmetic and copies ran while one was open for 0% -> 0% of each run, Pallas kernels for 0% -> 0%
where the time goes in v1:
time: 356 us
  Pallas kernels  339 us (95%)
  local copies, waits for them, and re-layouts  17.3 us (5%)
    pallas_call x1, Pallas kernels, step(): pl.pallas_call(functools.partial(kernel, n), name='mlp', out_shape=(jax.S...  339 us
    unnamed x1, local copies, waits for them, and re-layouts  17.3 us

profile of v1, /device:TPU:113, one launch (start us, length us, event | category | flops | bytes accessed | tf_op | source)
XLA Modules:
  0.0 356.3 jit_solution(804091395878480466)
XLA Ops:
  0.0 339.0 %mlp.1 = (bf16[2048,5120]{1,0:T(8,128)(2,1)}, bf16[4096,2560]{1,0:T(8,128)(2,1)}) custom-call(bf16[2048,5120]{1,0:T(8,128)(2,1)} %x_hbm.1, bf16[5120,4096]{1,0:T(8,128)(2,1)} %wg_hbm.1, bf16[5120,4096]{1,0:T(8,128)(2,1)} %wu_hbm.1, bf16[4096,5120]{1,0:T(8,128)(2,1)} %wd_hbm.1), custom_call_target="tpu_custom_call" | custom-call | flops 257698037760 | bytes 545259520 | tf_op jit(solution)/shard_map/mlp/pallas_call | solution.py:263
  339.0 17.3 %copy.6 = bf16[2048,5120]{1,0:T(8,128)(2,1)} copy(bf16[2048,5120]{1,0:T(8,128)(2,1)} %get-tuple-element.6) | data formatting | bytes 41943040

commit v2 on v0

v2 whole, which is shorter than its diff:
```python
import functools

import jax
import jax.numpy as jnp
from jax import lax
from jax.experimental import pallas as pl
from jax.experimental.pallas import tpu as pltpu
from jax.sharding import PartitionSpec as P

TILE = 512
MESH = pl.DeviceIdType.MESH
F32, BF16 = jnp.float32, jnp.bfloat16


def split(rows):
    big = rows * 9 // 32
    return big, rows // big, rows % big


def kernel(
    n, x_hbm, wg_hbm, wu_hbm, wd_hbm, y_hbm, far_hbm,
    x_buf, w_buf, hid, term, first, got1, second, got2, done,
    x_sem, w_sem, far_send, far_recv, hid_send, hid_recv,
    send1, recv1, send2, recv2, back2_send, back2_recv, back1_send, back1_recv,
    twin_send, local_sem, late_send, late_recv,
):
    rows, depth = x_hbm.shape
    width = wg_hbm.shape[1]
    half = depth // 2
    big, chunks, small = split(rows)
    ups, downs = width // TILE, half // TILE
    steps = ups + downs
    lanes = TILE // 2

    me = lax.axis_index("tp")
    chip, core = me // 2, me % 2
    twin = me + 1 - 2 * core
    inner, outer = ((chip + 1) // 2) % 2, chip // 2
    near, wrap = 2 * (chip + 1 - 2 * (chip % 2)) + core, 2 * (n // 2 - 1 - chip) + core
    keep, pick = (inner, outer), (outer, inner)
    peer1, peer2 = (near, wrap), (wrap, near)

    barrier = pltpu.get_barrier_semaphore()
    for peer in (near, wrap, twin):
        pl.semaphore_signal(barrier, inc=1, device_id={"tp": peer}, device_id_type=MESH)
    pl.semaphore_wait(barrier, 3)

    def remote(src, dst, send, recv, peer):
        return pltpu.make_async_remote_copy(
            src_ref=src, dst_ref=dst, send_sem=send, recv_sem=recv,
            device_id={"tp": peer}, device_id_type=MESH,
        )

    def tile(i):
        return pl.ds(pl.multiple_of(i * TILE, TILE), TILE)

    def far_copy(u):
        cols = pl.ds(pl.multiple_of((1 - core) * half + u * TILE, TILE), TILE)
        return remote(wd_hbm.at[:, cols], far_hbm.at[:, tile(u)], far_send.at[u], far_recv.at[u], twin)

    def x_copy(row, size):
        at = pl.multiple_of(row, 64)
        return pltpu.make_async_copy(x_hbm.at[pl.ds(at, size), :], x_buf.at[pl.ds(0, size)], x_sem)

    def up_copies(i, slot):
        return (
            pltpu.make_async_copy(wg_hbm.at[:, tile(i)], w_buf.at[slot, pl.ds(0, depth)], w_sem.at[slot, 0]),
            pltpu.make_async_copy(wu_hbm.at[:, tile(i)], w_buf.at[slot, pl.ds(depth, depth)], w_sem.at[slot, 1]),
        )

    def down_copies(u, slot):
        cols = pl.ds(pl.multiple_of(core * half + u * TILE, TILE), TILE)
        return (
            pltpu.make_async_copy(wd_hbm.at[:, cols], w_buf.at[slot, pl.ds(0, width)], w_sem.at[slot, 0]),
            pltpu.make_async_copy(far_hbm.at[:, tile(u)], w_buf.at[slot, pl.ds(width, width)], w_sem.at[slot, 1]),
        )

    def start(copies):
        for copy in copies:
            copy.start()

    def wait(copies):
        for copy in copies:
            copy.wait()

    def event(row, size, u, s):
        piece = size // 4

        def rows_of(h, q):
            return pl.multiple_of((2 * h + q) * piece, 16)

        def spot(d, h, q, count=1):
            cols = pl.multiple_of(core * half + u * TILE + d * lanes, lanes)
            return y_hbm.at[pl.ds(pl.multiple_of(row + (2 * h + q) * piece, 16), count * piece), pl.ds(cols, lanes)]

        def own(d, h, q, count=1):
            return term[u, pl.ds(rows_of(h, q), count * piece), pl.ds(d * lanes, lanes)]

        def part(d, q):
            return got1[d, u, pl.ds(pl.multiple_of(q * piece, 16), piece)].astype(F32)

        def out1(d):
            cut = pl.ds(0, 2 * piece)
            return remote(first.at[d, u, cut], got1.at[d, u, cut], send1.at[d, u], recv1.at[d, u], peer1[d])

        def out2(d):
            cut = pl.ds(0, piece)
            return remote(second.at[d, u, cut], got2.at[d, u, cut], send2.at[d, u], recv2.at[d, u], peer2[d])

        def mine(d):
            return done.at[d, u, pl.ds(0, piece)], spot(d, keep[d], pick[d])

        def back2(d):
            return remote(*mine(d), back2_send.at[d, u], back2_recv.at[d, u], peer2[d])

        def back1(d, q):
            src, dst = mine(d)
            if q:
                src = dst = spot(d, keep[d], 1 - pick[d])
            return remote(src, dst, back1_send.at[d, u, q], back1_recv.at[d, u, q], peer1[d])

        def to_twin(d):
            return remote(*mine(d), twin_send.at[d, u], late_recv, twin)

        def local(d):
            return pltpu.make_async_copy(*mine(d), local_sem.at[d, u])

        if s == 0:
            for d in range(2):
                first[d, u, pl.ds(0, 2 * piece)] = own(d, 1 - keep[d], 0, 2).astype(BF16)
            for d in range(2):
                out1(d).start()
        elif s == 1:
            for d in range(2):
                out1(d).wait_recv()
                q = 1 - pick[d]
                second[d, u, pl.ds(0, piece)] = (part(d, q) + own(d, keep[d], q)).astype(BF16)
            for d in range(2):
                out2(d).start()
        elif s == 2:
            for d in range(2):
                out2(d).wait_recv()
                total = part(d, pick[d]) + own(d, keep[d], pick[d]) + got2[d, u, pl.ds(0, piece)].astype(F32)
                done[d, u, pl.ds(0, piece)] = total.astype(BF16)
            for d in range(2):
                back2(d).start()
                back1(d, 0).start()
                to_twin(d).start()
                local(d).start()
        elif s == 3:
            for d in range(2):
                back2(d).wait_recv()
                back1(d, 1).start()
                here = spot(d, keep[d], 1 - pick[d])
                remote(here, here, late_send, late_recv, twin).start()
        else:
            for d in range(2):
                back1(d, 0).wait_recv()
                back1(d, 1).wait_recv()
                here = spot(d, 1 - keep[d], 0, 2)
                remote(here, here, late_send, late_recv, twin).start()
            for d in range(2):
                out1(d).wait_send()
                out2(d).wait_send()
                back2(d).wait_send()
                back1(d, 0).wait_send()
                back1(d, 1).wait_send()
                to_twin(d).wait_send()
                local(d).wait()

    def events(row, size, tau):
        for s in range(4, -1, -1):
            u = tau - 2 * s

            @pl.when((u >= 0) & (u < downs))
            def _(u=u, s=s):
                event(row, size, u, s)

    def chunk(k, row, size, before, after):
        x_copy(row, size).wait()
        par = k % 2
        base = k * steps
        here = pl.ds(0, size)

        def hid_copy(i):
            far = pl.ds(pl.multiple_of(width + i * TILE, TILE), TILE)
            return remote(
                hid.at[par, here, tile(i)], hid.at[par, here, far], hid_send.at[par], hid_recv.at[par], twin
            )

        def next_down(u, slot):
            @pl.when(k == 0)
            def _():
                far_copy(u).wait()

            start(down_copies(u, slot))

        def up_body(i, _):
            slot = (base + i) % 2
            wait(up_copies(i, slot))

            @pl.when(i < ups - 1)
            def _():
                start(up_copies(i + 1, 1 - slot))

            @pl.when(i == ups - 1)
            def _():
                next_down(0, 1 - slot)

            gate = jnp.dot(x_buf[here], w_buf[slot, pl.ds(0, depth)], preferred_element_type=F32)
            up = jnp.dot(x_buf[here], w_buf[slot, pl.ds(depth, depth)], preferred_element_type=F32)
            hid[par, here, tile(i)] = (jax.nn.silu(gate) * up).astype(BF16)
            before(i + downs)
            hid_copy(i).start()
            return _

        lax.fori_loop(0, ups, up_body, None)

        def down_step(u, lead):
            slot = (base + ups + u) % 2
            wait(down_copies(u, slot))
            if lead:
                next_down(u + 1, 1 - slot)
                if after is not None:
                    after()
                term[u, here] = jnp.dot(
                    hid[par, here, pl.ds(0, width)], w_buf[slot, pl.ds(0, width)], preferred_element_type=F32
                )
                remote(
                    hid.at[par, here, pl.ds(0, width)], hid.at[par, here, pl.ds(width, width)],
                    hid_send.at[par], hid_recv.at[par], twin,
                ).wait()
                term[u, here] += jnp.dot(
                    hid[par, here, pl.ds(width, width)], w_buf[slot, pl.ds(width, width)],
                    preferred_element_type=F32,
                )
            else:
                @pl.when(u < downs - 1)
                def _():
                    next_down(u + 1, 1 - slot)

                if after is not None:
                    @pl.when(u == downs - 1)
                    def _():
                        start(up_copies(0, 1 - slot))

                term[u, here] = jnp.dot(
                    hid[par, here], w_buf[slot, pl.ds(0, 2 * width)], preferred_element_type=F32
                )
            events(row, size, u)

        down_step(0, True)

        def down_body(u, _):
            down_step(u, False)
            return _

        lax.fori_loop(1, downs, down_body, None)

    start(up_copies(0, 0))
    x_copy(0, big).start()
    for u in range(downs):
        far_copy(u).start()

    def chunk_body(k, _):
        row = k * big

        def before(tau):
            @pl.when(k > 0)
            def _():
                events(row - big, big, tau)

        def after():
            @pl.when(k < chunks - 1)
            def _():
                x_copy(row + big, big).start()

            @pl.when(k == chunks - 1)
            def _():
                x_copy(row + big, small).start()

        chunk(k, row, big, before, after)
        return _

    lax.fori_loop(0, chunks, chunk_body, None)
    row = chunks * big
    chunk(chunks, row, small, lambda tau: events(row - big, big, tau), None)

    def tail(tau, _):
        events(row, small, tau)
        return _

    lax.fori_loop(downs, downs + 8, tail, None)

    share = rows // 4 * 3
    sent = y_hbm.at[pl.ds(0, share), pl.ds(0, half)]
    pltpu.make_async_copy(sent, sent, late_send).wait()
    whole = y_hbm.at[:, pl.ds(0, half)]
    pltpu.make_async_copy(whole, whole, late_recv).wait()


def solution(mesh):
    n = mesh.shape["tp"]

    def step(x, w_gate, w_up, w_down):
        rows, depth = x.shape
        width = w_gate.shape[1]
        half = depth // 2
        downs = half // TILE
        big = split(rows)[0]
        piece, lanes = big // 4, TILE // 2
        dma = pltpu.SemaphoreType.DMA
        y, _ = pl.pallas_call(
            functools.partial(kernel, n),
            name="mlp",
            out_shape=(
                jax.ShapeDtypeStruct((rows, depth), BF16),
                jax.ShapeDtypeStruct((width, half), BF16),
            ),
            in_specs=[pl.BlockSpec(memory_space=pl.ANY)] * 4,
            out_specs=[pl.BlockSpec(memory_space=pl.ANY)] * 2,
            scratch_shapes=[
                pltpu.VMEM((big, depth), BF16),
                pltpu.VMEM((2, 2 * depth, TILE), BF16),
                pltpu.VMEM((2, big, 2 * width), BF16),
                pltpu.VMEM((downs, big, TILE), F32),
                pltpu.VMEM((2, downs, 2 * piece, lanes), BF16),
                pltpu.VMEM((2, downs, 2 * piece, lanes), BF16),
                pltpu.VMEM((2, downs, piece, lanes), BF16),
                pltpu.VMEM((2, downs, piece, lanes), BF16),
                pltpu.VMEM((2, downs, piece, lanes), BF16),
                dma,
                dma((2, 2)),
                dma((downs,)),
                dma((downs,)),
                dma((2,)),
                dma((2,)),
                dma((2, downs)),
                dma((2, downs)),
                dma((2, downs)),
                dma((2, downs)),
                dma((2, downs)),
                dma((2, downs)),
                dma((2, downs, 2)),
                dma((2, downs, 2)),
                dma((2, downs)),
                dma((2, downs)),
                dma,
                dma,
            ],
            compiler_params=pltpu.CompilerParams(
                collective_id=0, has_side_effects=True, vmem_limit_bytes=67_043_328
            ),
            cost_estimate=pl.CostEstimate(
                flops=6 * rows * depth * width,
                bytes_accessed=2 * (2 * rows * depth + 12 * depth * width),
                transcendentals=rows * width,
            ),
        )(x, w_gate, w_up, w_down)
        return y

    return jax.shard_map(
        step,
        mesh=mesh,
        in_specs=(P("dp", None), P(None, "tp"), P(None, "tp"), P("tp", None)),
        out_specs=P("dp", None),
        check_vma=False,
    )
```

time: 546 us -> 340 us (0.62)
  Pallas kernels: 0 us -> 322 us
  matrix products: 298 us -> 0 us
  waiting for transfers between devices: 217 us -> 0 us
  between operations: 13.4 us -> 0.01 us
    pallas_call x0 -> x1, Pallas kernels: none -> 322 us  [step(): pl.pallas_call(functools.partial(kernel, n), name='mlp', out_shape=(jax.S...]
    dot_general x3 -> x0, matrix products: 298 us -> none  [the longest x1 105 us: step(): up = jnp.dot(x, w_up, preferred_element_type=jnp.float32)]
    psum x1 -> x0, waiting for transfers between devices: 217 us -> none  [step(): return lax.psum(term, 'tp')]
  transfers between devices with their start and end apart: 1 -> 0, of which waited for: 1 -> 0; matrix products, arithmetic and copies ran while one was open for 0% -> 0% of each run, Pallas kernels for 0% -> 0%
where the time goes in v2:
time: 340 us
  Pallas kernels  322 us (95%)
  local copies, waits for them, and re-layouts  17.3 us (5%)
    pallas_call x1, Pallas kernels, step(): pl.pallas_call(functools.partial(kernel, n), name='mlp', out_shape=(jax.S...  322 us
    unnamed x1, local copies, waits for them, and re-layouts  17.3 us

profile of v2, /device:TPU:113, one launch (start us, length us, event | category | flops | bytes accessed | tf_op | source)
XLA Modules:
  0.0 339.5 jit_solution(8885667325381657850)
XLA Ops:
  0.0 322.2 %mlp.1 = (bf16[2048,5120]{1,0:T(8,128)(2,1)}, bf16[4096,2560]{1,0:T(8,128)(2,1)}) custom-call(bf16[2048,5120]{1,0:T(8,128)(2,1)} %x_hbm.1, bf16[5120,4096]{1,0:T(8,128)(2,1)} %wg_hbm.1, bf16[5120,4096]{1,0:T(8,128)(2,1)} %wu_hbm.1, bf16[4096,5120]{1,0:T(8,128)(2,1)} %wd_hbm.1), custom_call_target="tpu_custom_call" | custom-call | flops 257698037760 | bytes 545259520 | tf_op jit(solution)/shard_map/mlp/pallas_call | solution.py:313
  322.2 17.3 %copy.6 = bf16[2048,5120]{1,0:T(8,128)(2,1)} copy(bf16[2048,5120]{1,0:T(8,128)(2,1)} %get-tuple-element.6) | data formatting | bytes 41943040

commit v3 on v2

--- a/solution.py
+++ b/solution.py
@@ -12,22 +12,26 @@
 F32, BF16 = jnp.float32, jnp.bfloat16
 
 
+SHARES = ((9, 2), (8, 1), (6, 1))
+BLOCKS = 16
+GAP, LAST_GAP = 3, 2
+
+
 def split(rows):
-    big = rows * 9 // 32
-    return big, rows // big, rows % big
+    return [(rows * share // 32, count) for share, count in SHARES]
 
 
 def kernel(
     n, x_hbm, wg_hbm, wu_hbm, wd_hbm, y_hbm, far_hbm,
-    x_buf, w_buf, hid, term, first, got1, second, got2, done,
+    x_buf, w_buf, hid, far_hid, term, first, got1, second, got2, done,
     x_sem, w_sem, far_send, far_recv, hid_send, hid_recv,
     send1, recv1, send2, recv2, back2_send, back2_recv, back1_send, back1_recv,
-    twin_send, local_sem, late_send, late_recv,
+    local_sem, late_send, late_recv,
 ):
     rows, depth = x_hbm.shape
     width = wg_hbm.shape[1]
     half = depth // 2
-    big, chunks, small = split(rows)
+    groups = split(rows)
     ups, downs = width // TILE, half // TILE
     steps = ups + downs
     lanes = TILE // 2
@@ -40,11 +44,6 @@
     keep, pick = (inner, outer), (outer, inner)
     peer1, peer2 = (near, wrap), (wrap, near)
 
-    barrier = pltpu.get_barrier_semaphore()
-    for peer in (near, wrap, twin):
-        pl.semaphore_signal(barrier, inc=1, device_id={"tp": peer}, device_id_type=MESH)
-    pl.semaphore_wait(barrier, 3)
-
     def remote(src, dst, send, recv, peer):
         return pltpu.make_async_remote_copy(
             src_ref=src, dst_ref=dst, send_sem=send, recv_sem=recv,
@@ -119,8 +118,10 @@
                 src = dst = spot(d, keep[d], 1 - pick[d])
             return remote(src, dst, back1_send.at[d, u, q], back1_recv.at[d, u, q], peer1[d])
 
-        def to_twin(d):
-            return remote(*mine(d), twin_send.at[d, u], late_recv, twin)
+        def to_twin():
+            cols = pl.ds(pl.multiple_of(core * half + u * TILE, TILE), TILE)
+            here = y_hbm.at[pl.ds(pl.multiple_of(row, 64), size), cols]
+            return remote(here, here, late_send, late_recv, twin)
 
         def local(d):
             return pltpu.make_async_copy(*mine(d), local_sem.at[d, u])
@@ -145,32 +146,30 @@
             for d in range(2):
                 back2(d).start()
                 back1(d, 0).start()
-                to_twin(d).start()
                 local(d).start()
         elif s == 3:
             for d in range(2):
                 back2(d).wait_recv()
                 back1(d, 1).start()
-                here = spot(d, keep[d], 1 - pick[d])
-                remote(here, here, late_send, late_recv, twin).start()
         else:
             for d in range(2):
                 back1(d, 0).wait_recv()
                 back1(d, 1).wait_recv()
-                here = spot(d, 1 - keep[d], 0, 2)
-                remote(here, here, late_send, late_recv, twin).start()
+                local(d).wait()
+            to_twin().start()
             for d in range(2):
                 out1(d).wait_send()
                 out2(d).wait_send()
                 back2(d).wait_send()
                 back1(d, 0).wait_send()
                 back1(d, 1).wait_send()
-                to_twin(d).wait_send()
-                local(d).wait()
+
+    def gap_of(size):
+        return LAST_GAP if size == groups[-1][0] else GAP
 
     def events(row, size, tau):
         for s in range(4, -1, -1):
-            u = tau - 2 * s
+            u = tau - gap_of(size) * s
 
             @pl.when((u >= 0) & (u < downs))
             def _(u=u, s=s):
@@ -183,9 +182,8 @@
         here = pl.ds(0, size)
 
         def hid_copy(i):
-            far = pl.ds(pl.multiple_of(width + i * TILE, TILE), TILE)
             return remote(
-                hid.at[par, here, tile(i)], hid.at[par, here, far], hid_send.at[par], hid_recv.at[par], twin
+                hid.at[here, tile(i)], far_hid.at[par, here, tile(i)], hid_send.at[par], hid_recv.at[par], twin
             )
 
         def next_down(u, slot):
@@ -209,7 +207,7 @@
 
             gate = jnp.dot(x_buf[here], w_buf[slot, pl.ds(0, depth)], preferred_element_type=F32)
             up = jnp.dot(x_buf[here], w_buf[slot, pl.ds(depth, depth)], preferred_element_type=F32)
-            hid[par, here, tile(i)] = (jax.nn.silu(gate) * up).astype(BF16)
+            hid[here, tile(i)] = (jax.nn.silu(gate) * up).astype(BF16)
             before(i + downs)
             hid_copy(i).start()
             return _
@@ -224,15 +222,13 @@
                 if after is not None:
                     after()
                 term[u, here] = jnp.dot(
-                    hid[par, here, pl.ds(0, width)], w_buf[slot, pl.ds(0, width)], preferred_element_type=F32
+                    hid[here], w_buf[slot, pl.ds(0, width)], preferred_element_type=F32
                 )
                 remote(
-                    hid.at[par, here, pl.ds(0, width)], hid.at[par, here, pl.ds(width, width)],
-                    hid_send.at[par], hid_recv.at[par], twin,
+                    hid.at[here], far_hid.at[par, here], hid_send.at[par], hid_recv.at[par], twin,
                 ).wait()
                 term[u, here] += jnp.dot(
-                    hid[par, here, pl.ds(width, width)], w_buf[slot, pl.ds(width, width)],
-                    preferred_element_type=F32,
+                    far_hid[par, here], w_buf[slot, pl.ds(width, width)], preferred_element_type=F32
                 )
             else:
                 @pl.when(u < downs - 1)
@@ -245,8 +241,11 @@
                         start(up_copies(0, 1 - slot))
 
                 term[u, here] = jnp.dot(
-                    hid[par, here], w_buf[slot, pl.ds(0, 2 * width)], preferred_element_type=F32
+                    hid[here], w_buf[slot, pl.ds(0, width)], preferred_element_type=F32
+                ) + jnp.dot(
+                    far_hid[par, here], w_buf[slot, pl.ds(width, width)], preferred_element_type=F32
                 )
+            before(steps + u)
             events(row, size, u)
 
         down_step(0, True)
@@ -257,46 +256,89 @@
 
         lax.fori_loop(1, downs, down_body, None)
 
+    x_copy(0, groups[0][0]).start()
     start(up_copies(0, 0))
-    x_copy(0, big).start()
+    barrier = pltpu.get_barrier_semaphore()
+    for peer in (near, wrap, twin):
+        pl.semaphore_signal(barrier, inc=1, device_id={"tp": peer}, device_id_type=MESH)
+    pl.semaphore_wait(barrier, 3)
     for u in range(downs):
         far_copy(u).start()
 
-    def chunk_body(k, _):
-        row = k * big
-
-        def before(tau):
-            @pl.when(k > 0)
-            def _():
-                events(row - big, big, tau)
-
-        def after():
-            @pl.when(k < chunks - 1)
-            def _():
-                x_copy(row + big, big).start()
-
-            @pl.when(k == chunks - 1)
-            def _():
-                x_copy(row + big, small).start()
-
-        chunk(k, row, big, before, after)
+    def idle(tau):
+        return
+
+    first_chunk, row, before = 0, 0, idle
+    for g, (size, count) in enumerate(groups):
+        later = groups[g + 1][0] if g + 1 < len(groups) else None
+
+        def one(k, at, first_in_group, before=before, size=size, later=later, end=first_chunk + count - 1):
+            def after():
+                if later is None:
+                    if count > 1:
+                        @pl.when(k < end)
+                        def _():
+                            x_copy(at + size, size).start()
+                    return
+
+                @pl.when(k < end)
+                def _():
+                    x_copy(at + size, size).start()
+
+                @pl.when(k == end)
+                def _():
+                    x_copy(at + size, later).start()
+
+            chunk(k, at, size, before, None if later is None and count == 1 else after)
+
+        if count == 1:
+            one(first_chunk, row, True)
+        else:
+            assert g == 0
+
+            def body(k, _, size=size, one=one):
+                at = k * size
+
+                def before(tau):
+                    @pl.when(k > 0)
+                    def _():
+                        events(at - size, size, tau)
+
+                one(k, at, False, before=before)
+                return _
+
+            lax.fori_loop(0, count, body, None)
+        row += size * count
+        first_chunk += count
+        before = functools.partial(events, row - size, size)
+
+    def tail(tau, _):
+        before(tau)
         return _
 
-    lax.fori_loop(0, chunks, chunk_body, None)
-    row = chunks * big
-    chunk(chunks, row, small, lambda tau: events(row - big, big, tau), None)
-
-    def tail(tau, _):
-        events(row, small, tau)
-        return _
-
-    lax.fori_loop(downs, downs + 8, tail, None)
-
-    share = rows // 4 * 3
-    sent = y_hbm.at[pl.ds(0, share), pl.ds(0, half)]
-    pltpu.make_async_copy(sent, sent, late_send).wait()
+    lax.fori_loop(downs, downs + 4 * LAST_GAP, tail, None)
+
     whole = y_hbm.at[:, pl.ds(0, half)]
+    pltpu.make_async_copy(whole, whole, late_send).wait()
     pltpu.make_async_copy(whole, whole, late_recv).wait()
+
+
+def copy_kernel(src, dst, buf, read_sem, write_sem):
+    size = src.shape[0] // BLOCKS
+
+    def read(i):
+        return pltpu.make_async_copy(src.at[pl.ds(i * size, size)], buf.at[i], read_sem.at[i])
+
+    def write(i):
+        return pltpu.make_async_copy(buf.at[i], dst.at[pl.ds(i * size, size)], write_sem.at[i])
+
+    for i in range(BLOCKS):
+        read(i).start()
+    for i in range(BLOCKS):
+        read(i).wait()
+        write(i).start()
+    for i in range(BLOCKS):
+        write(i).wait()
 
 
 def solution(mesh):
@@ -307,7 +349,7 @@
         width = w_gate.shape[1]
         half = depth // 2
         downs = half // TILE
-        big = split(rows)[0]
+        big = max(split(rows))[0]
         piece, lanes = big // 4, TILE // 2
         dma = pltpu.SemaphoreType.DMA
         y, _ = pl.pallas_call(
@@ -322,7 +364,8 @@
             scratch_shapes=[
                 pltpu.VMEM((big, depth), BF16),
                 pltpu.VMEM((2, 2 * depth, TILE), BF16),
-                pltpu.VMEM((2, big, 2 * width), BF16),
+                pltpu.VMEM((big, width), BF16),
+                pltpu.VMEM((2, big, width), BF16),
                 pltpu.VMEM((downs, big, TILE), F32),
                 pltpu.VMEM((2, downs, 2 * piece, lanes), BF16),
                 pltpu.VMEM((2, downs, 2 * piece, lanes), BF16),
@@ -344,7 +387,6 @@
                 dma((2, downs, 2)),
                 dma((2, downs, 2)),
                 dma((2, downs)),
-                dma((2, downs)),
                 dma,
                 dma,
             ],
@@ -357,7 +399,16 @@
                 transcendentals=rows * width,
             ),
         )(x, w_gate, w_up, w_down)
-        return y
+        return pl.pallas_call(
+            copy_kernel,
+            name="hand_over",
+            out_shape=jax.ShapeDtypeStruct((rows, depth), BF16),
+            in_specs=[pl.BlockSpec(memory_space=pl.ANY)],
+            out_specs=pl.BlockSpec(memory_space=pl.ANY),
+            scratch_shapes=[pltpu.VMEM((BLOCKS, rows // BLOCKS, depth), BF16), dma((BLOCKS,)), dma((BLOCKS,))],
+            compiler_params=pltpu.CompilerParams(vmem_limit_bytes=67_043_328),
+            cost_estimate=pl.CostEstimate(flops=0, bytes_accessed=4 * rows * depth, transcendentals=0),
+        )(y)
 
     return jax.shard_map(
         step,

time: 340 us -> 329 us (0.968)
  local copies, waits for them, and re-layouts: 17.3 us -> 0 us
  Pallas kernels: 322 us -> 328 us
    unnamed x1 -> x0, local copies, waits for them, and re-layouts: 17.3 us -> none
    pallas_call x0 -> x1, Pallas kernels: none -> 14.7 us  [step(): pl.pallas_call(copy_kernel, name='hand_over', out_shape=jax.ShapeDtypeStr...]
    pallas_call x1, Pallas kernels: 322 us -> 314 us  [step(): pl.pallas_call(functools.partial(kernel, n), name='mlp', out_shape=(jax.S...]
where the time goes in v3:
time: 329 us
  Pallas kernels  328 us (100%)
    pallas_call x1, Pallas kernels, step(): pl.pallas_call(functools.partial(kernel, n), name='mlp', out_shape=(jax.S...  314 us
    pallas_call x1, Pallas kernels, step(): pl.pallas_call(copy_kernel, name='hand_over', out_shape=jax.ShapeDtypeStr...  14.7 us

profile of v3, /device:TPU:113, one launch (start us, length us, event | category | flops | bytes accessed | tf_op | source)
XLA Modules:
  0.0 328.6 jit_solution(2878682385131895380)
XLA Ops:
  0.0 313.7 %mlp.1 = (bf16[2048,5120]{1,0:T(8,128)(2,1)}, bf16[4096,2560]{1,0:T(8,128)(2,1)}) custom-call(bf16[2048,5120]{1,0:T(8,128)(2,1)} %x_hbm.1, bf16[5120,4096]{1,0:T(8,128)(2,1)} %wg_hbm.1, bf16[5120,4096]{1,0:T(8,128)(2,1)} %wu_hbm.1, bf16[4096,5120]{1,0:T(8,128)(2,1)} %wd_hbm.1), custom_call_target="tpu_custom_call" | custom-call | flops 257698037760 | bytes 545259520 | tf_op jit(solution)/shard_map/mlp/pallas_call | solution.py:355
  313.7 14.7 %hand_over.1 = bf16[2048,5120]{1,0:T(8,128)(2,1)} custom-call(bf16[2048,5120]{1,0:T(8,128)(2,1)} %get-tuple-element.6.src), custom_call_target="tpu_custom_call" | custom-call | bytes 41943040 | tf_op jit(solution)/shard_map/hand_over/pallas_call | solution.py:402

commit v4 on v3

--- a/solution.py
+++ b/solution.py
@@ -14,7 +14,7 @@
 
 SHARES = ((9, 2), (8, 1), (6, 1))
 BLOCKS = 16
-GAP, LAST_GAP = 3, 2
+GAP, LAST_GAP = 3, 3
 
 
 def split(rows):
@@ -23,7 +23,7 @@
 
 def kernel(
     n, x_hbm, wg_hbm, wu_hbm, wd_hbm, y_hbm, far_hbm,
-    x_buf, w_buf, hid, far_hid, term, first, got1, second, got2, done,
+    x_buf, w_buf, hid, far_hid, term, first, got1, second, got2, done, act,
     x_sem, w_sem, far_send, far_recv, hid_send, hid_recv,
     send1, recv1, send2, recv2, back2_send, back2_recv, back1_send, back1_recv,
     local_sem, late_send, late_recv,
@@ -206,8 +206,9 @@
                 next_down(0, 1 - slot)
 
             gate = jnp.dot(x_buf[here], w_buf[slot, pl.ds(0, depth)], preferred_element_type=F32)
+            act[here] = jax.nn.silu(gate)
             up = jnp.dot(x_buf[here], w_buf[slot, pl.ds(depth, depth)], preferred_element_type=F32)
-            hid[here, tile(i)] = (jax.nn.silu(gate) * up).astype(BF16)
+            hid[here, tile(i)] = (act[here] * up).astype(BF16)
             before(i + downs)
             hid_copy(i).start()
             return _
@@ -372,6 +373,7 @@
                 pltpu.VMEM((2, downs, piece, lanes), BF16),
                 pltpu.VMEM((2, downs, piece, lanes), BF16),
                 pltpu.VMEM((2, downs, piece, lanes), BF16),
+                pltpu.VMEM((big, TILE), F32),
                 dma,
                 dma((2, 2)),
                 dma((downs,)),

time: 329 us -> 329 us (level)
  no operation moved by 1% of the time
where the time goes in v4:
time: 329 us; the launch traced here: 328 us
  Pallas kernels  328 us (100%)
    pallas_call x1, Pallas kernels, step(): pl.pallas_call(functools.partial(kernel, n), name='mlp', out_shape=(jax.S...  314 us
    pallas_call x1, Pallas kernels, step(): pl.pallas_call(copy_kernel, name='hand_over', out_shape=jax.ShapeDtypeStr...  14.7 us

profile of v4, /device:TPU:113, one launch (start us, length us, event | category | flops | bytes accessed | tf_op | source)
XLA Modules:
  0.0 328.5 jit_solution(5440428614673047920)
XLA Ops:
  0.0 313.5 %mlp.1 = (bf16[2048,5120]{1,0:T(8,128)(2,1)}, bf16[4096,2560]{1,0:T(8,128)(2,1)}) custom-call(bf16[2048,5120]{1,0:T(8,128)(2,1)} %x_hbm.1, bf16[5120,4096]{1,0:T(8,128)(2,1)} %wg_hbm.1, bf16[5120,4096]{1,0:T(8,128)(2,1)} %wu_hbm.1, bf16[4096,5120]{1,0:T(8,128)(2,1)} %wd_hbm.1), custom_call_target="tpu_custom_call" | custom-call | flops 257698037760 | bytes 545259520 | tf_op jit(solution)/shard_map/mlp/pallas_call | solution.py:356
  313.5 14.7 %hand_over.1 = bf16[2048,5120]{1,0:T(8,128)(2,1)} custom-call(bf16[2048,5120]{1,0:T(8,128)(2,1)} %get-tuple-element.6.src), custom_call_target="tpu_custom_call" | custom-call | bytes 41943040 | tf_op jit(solution)/shard_map/hand_over/pallas_call | solution.py:404
